TPU v7x, 256 devices: a whole 4x4x8 slice. The times are simulated.
256 devices in a mesh: dp: 8 (over z), expert: 32 (over x, y, core).
Axes of the slice: x: 4, y: 4, z: 8, core: 2. Of those that a mesh axis runs over, the one named last changes fastest.
Arguments:
- tokens: bfloat16 [2048, 7168], P('expert'), may hold values from -6 to 6
- routes: int32 [2048, 8], P('expert'), may hold values from 0 to 31, all different within a row; in each aligned block of 64 rows (0 to 63, 64 to 127, ...) at most 20 rows name the same one
- route_weight: int32 [2048, 8], P('expert'), may hold values from 1 to 4096
- w_gate: bfloat16 [32, 7168, 2048], P('expert', None, 'dp'), may hold values from -0.0625 to 0.0625
- w_up: bfloat16 [32, 7168, 2048], P('expert', None, 'dp'), may hold values from -0.0625 to 0.0625
- w_down: bfloat16 [32, 2048, 7168], P('expert', 'dp'), may hold values from -0.125 to 0.125
- prev_inputs: bfloat16 [8, 32, 64, 7168], P('dp', 'expert'), may hold values from -6 to 6
Outputs:
- mixed: bfloat16 [2048, 7168], P('expert', 'dp')
- hessian: float32 [7168, 32, 128], P('dp', 'expert')
Inputs may be any that keep to these rules, and one draw needn't show every extreme that they name: `routes`: in each aligned block of 64 rows (the rows of one index of expert) no expert is named more than 20 times, a bound that some block reaches; the 8 experts of a token differ.
All inputs are finite; a program needn't handle non-finite values.
Results may differ from a plain program's by a relative error of at most 0.014.
Values may be sent and summed in bfloat16 or wider, within the bound.
A program may use at most 128 MiB of HBM per device.

v0:
```python
import jax
import jax.numpy as jnp
from jax import lax
from jax.sharding import PartitionSpec as P

HESS_COLS = 128


def split_up(value, dim, length):
    before, after = (value.shape[:dim], value.shape[dim + 1 :])
    return jnp.moveaxis(value.reshape(*before, length, -1, *after), dim, 0)


def summed_on_arrival(value, axis, dim):
    blocks = split_up(value, dim, lax.axis_size(axis))
    arrived = lax.all_to_all(blocks, axis, split_axis=0, concat_axis=0, tiled=True)
    return arrived.astype(jnp.float32).sum(axis=0)


def route_slots(flat_ids, experts_all):
    onehot = (flat_ids[:, None] == jnp.arange(experts_all, dtype=jnp.int32)[None, :]).astype(
        jnp.int32
    )
    earlier = jnp.cumsum(onehot, axis=0) - onehot
    return jnp.sum(earlier * onehot, axis=1)


def combine_rows(back, places, shares, tok_dev, top):
    columns = back.shape[-1]
    rows = back.reshape(-1, columns)[places]
    weighted = rows.astype(jnp.float32) * shares.reshape(-1, 1)
    return jnp.sum(weighted.reshape(tok_dev, top, columns), axis=1)


def shards(tokens, routes, route_weight, w_gate, w_up, w_down, prev_inputs):
    tok_dev, top = routes.shape
    exp_dev = w_gate.shape[0]
    width = tokens.shape[1]
    n_expert = lax.axis_size("expert")
    n_dp = lax.axis_size("dp")
    experts_all = exp_dev * n_expert
    capacity = min(tok_dev, tok_dev * top * 5 // (4 * experts_all))
    col_width = width // n_dp
    flat_ids = routes.reshape(-1)
    slots = route_slots(flat_ids, experts_all)
    places = flat_ids * capacity + slots
    weight_counts = route_weight.astype(jnp.float32)
    shares = 2.5 * weight_counts / jnp.sum(weight_counts, axis=1, keepdims=True)
    picks = jnp.arange(experts_all * capacity, dtype=jnp.int32)[:, None] == places[None, :]
    placing = jnp.any(picks.reshape(experts_all * capacity, tok_dev, top), axis=2).astype(
        jnp.bfloat16
    )
    my_cols = lax.dynamic_slice_in_dim(tokens, lax.axis_index("dp") * col_width, col_width, 1)
    outgoing = jnp.dot(placing, my_cols, preferred_element_type=jnp.float32).astype(jnp.bfloat16)
    outgoing = outgoing.reshape(experts_all, capacity, col_width)
    arrived = lax.all_to_all(outgoing, "expert", split_axis=0, concat_axis=0, tiled=True)
    arrived = arrived.reshape(n_expert, exp_dev, capacity, col_width)
    piece = lax.all_gather(arrived, "dp", axis=3, tiled=True)
    gate_add = jnp.einsum("sjcd,jdf->sjcf", piece, w_gate, preferred_element_type=jnp.float32)
    up_add = jnp.einsum("sjcd,jdf->sjcf", piece, w_up, preferred_element_type=jnp.float32)
    history = prev_inputs.reshape(prev_inputs.shape[1], prev_inputs.shape[2], width)
    head_cols = history[:, :, :HESS_COLS]
    gram_scale = 2.0 / (n_dp * history.shape[1])
    hessian = lax.psum_scatter(
        (
            jnp.einsum("jrd,jrh->djh", history, head_cols, preferred_element_type=jnp.float32)
            * gram_scale
        ).astype(jnp.bfloat16),
        "dp",
        scatter_dimension=0,
        tiled=True,
    ).astype(jnp.float32)
    hidden = (jax.nn.silu(gate_add) * up_add).astype(jnp.bfloat16)
    partial_out = jnp.einsum("sjcf,jfd->sjcd", hidden, w_down, preferred_element_type=jnp.float32)
    partial_out = partial_out.astype(jnp.bfloat16)
    back = lax.all_to_all(
        partial_out.reshape(experts_all, capacity, width),
        "expert",
        split_axis=0,
        concat_axis=0,
        tiled=True,
    )
    own_sum = combine_rows(back, places, shares, tok_dev, top)
    mixed = summed_on_arrival(own_sum.astype(jnp.bfloat16), "dp", 1)
    return (mixed.astype(jnp.bfloat16), hessian)


def solution(mesh):
    placed = (
        P("expert", None),
        P("expert", None),
        P("expert", None),
        P("expert", None, "dp"),
        P("expert", None, "dp"),
        P("expert", "dp", None),
        P("dp", "expert", None, None),
    )
    return jax.shard_map(
        shards,
        mesh=mesh,
        in_specs=placed,
        out_specs=(P("expert", "dp"), P("dp", "expert", None)),
        check_vma=False,
    )
```

profile of v0, /device:TPU:13, one launch (start us, length us, event | category | flops | bytes accessed | tf_op | source)
XLA Modules:
  0.0 430.2 jit_solution(2899087094357470166)
XLA Ops:
  7.2 0.0 copy-start
  7.2 0.0 all-gather.3.cloned.1.call-start
  7.2 0.8 copy.38
  8.1 0.1 eq.44
  8.2 0.1 eq.40
  8.3 1.2 reduce-window.6
  9.4 0.2 slice_reduce_fusion
  9.7 0.1 fusion.28
  9.8 0.1 reduce_sum.44
  9.9 0.5 fusion.8
  10.4 0.0 copy-done
  10.4 0.5 convolution_convert_fusion.1
  10.9 0.3 reshape.127
  11.2 25.7 %all_to_all.15 = bf16[32,20,896]{2,1,0:T(8,128)(2,1)S(1)} all-to-all(bf16[32,20,896]{2,1,0:T(8,128)(2,1)S(1)} %reshape.127), channel_id=1, replica_groups=mesh['dp'=8,'expert'=32] {'expert'}, dimensions={0} | all-to-all | bytes 2293760 | tf_op jit(solution)/shard_map/all_to_all | solution.py:56
  36.9 1.1 copy.42
  38.1 0.0 all-gather.3.cloned.1.call-update
  38.1 102.8 %all-gather.3.cloned.1.call-done = bf16[32,20,7168]{2,0,1:T(8,128)(2,1)} async-done(((bf16[32,20,896]{2,0,1:T(8,128)(2,1)}), bf16[32,20,7168]{2,0,1:T(8,128)(2,1)}) %all-gather.3.cloned.1.call-update) | async-done | bytes 9175056 | tf_op jit(solution)/shard_map/all_gather | solution.py:58
  140.9 7.3 %fusion.9 = f32[32,1,20,256]{3,0,2,1:T(8,128)S(1)} fusion(bf16[32,20,7168]{2,0,1:T(8,128)(2,1)} %all-gather.3.cloned.1.call-done, bf16[1,7168,256]{2,1,0:T(8,128)(2,1)} %param.10), kind=kOutput, calls=%fused_computation.15 | convolution fusion | flops 2348810240 | bytes 13500416 | tf_op jit(solution)/shard_map/sjcd,jdf->sjcf/dot_general | solution.py:59
  148.2 0.0 copy-done.5
  148.2 1.0 copy-done.6
  149.2 2.5 fusion.21
  151.7 0.0 copy-done.2
  151.8 6.1 %convolution_convert_fusion = bf16[32,20,7168]{2,0,1:T(8,128)(2,1)} fusion(bf16[32,20,256]{2,0,1:T(8,128)(2,1)S(1)} %fusion.21, bf16[1,256,7168]{2,1,0:T(8,128)(2,1)S(1)} %copy-done.2), kind=kOutput, calls=%fused_computation.3 | convolution fusion | flops 2353397760 | bytes 13172736 | tf_op jit(solution)/shard_map/sjcf,jfd->sjcd/dot_general | solution.py:74
  157.8 13.0 %copy.43 = bf16[32,20,7168]{2,1,0:T(8,128)(2,1)} copy(bf16[32,20,7168]{2,0,1:T(8,128)(2,1)} %convolution_convert_fusion) | data formatting | bytes 18350080 | tf_op jit(solution)/shard_map/convert_element_type | solution.py:75
  170.8 8.0 %all-to-all-start.1 = ((bf16[32,20,7168]{2,1,0:T(8,128)(2,1)}), bf16[32,20,7168]{2,1,0:T(8,128)(2,1)}, u32[]{:S(2)}, u32[]{:S(2)}) async-start(bf16[32,20,7168]{2,1,0:T(8,128)(2,1)} %copy.43), calls=%async_computation.1 | async-start | bytes 22020096 | tf_op jit(solution)/shard_map/all_to_all | solution.py:76
  178.9 0.0 reduce-scatter.4.cloned.1.call-start
  178.9 0.0 copy-done.3
  178.9 0.0 copy-start.4
  178.9 0.7 fusion.2
  179.6 2.3 copy.49
  181.9 0.0 reduce-scatter.4.cloned.1.call-update
  182.0 0.1 mul.62
  182.0 0.0 copy-done.4
  182.1 0.1 copy.44
  182.2 167.9 %all-to-all-done.1 = bf16[32,20,7168]{2,1,0:T(8,128)(2,1)} async-done(((bf16[32,20,7168]{2,1,0:T(8,128)(2,1)}), bf16[32,20,7168]{2,1,0:T(8,128)(2,1)}, u32[]{:S(2)}, u32[]{:S(2)}) %all-to-all-start.1) | async-done | bytes 9175072 | tf_op jit(solution)/shard_map/all_to_all | solution.py:76
  350.1 13.3 %reshape.134 = bf16[640,7168]{1,0:T(8,128)(2,1)} reshape(bf16[32,20,7168]{2,1,0:T(8,128)(2,1)} %all-to-all-done.1) | data formatting | bytes 18350080 | tf_op jit(solution)/shard_map/reshape | solution.py:30
  363.4 18.6 %gather_fusion = bf16[512,7168]{1,0:T(8,128)(2,1)} fusion(bf16[640,7168]{1,0:T(8,128)(2,1)} %reshape.134, s32[1024]{0:T(1024)S(1)} %pad_clamp_fusion), kind=kCustom, calls=%fused_computation | custom fusion | bytes 14682112 | tf_op jit(solution)/shard_map/gather | solution.py:30
  382.0 8.9 %fusion = bf16[64,7168]{1,0:T(8,128)(2,1)S(1)} fusion(bf16[512,7168]{1,0:T(8,128)(2,1)} %gather_fusion, f32[64,8]{1,0:T(8,128)S(1)} %copy.44), kind=kLoop, calls=%fused_computation.2 | loop fusion | flops 10551296 | bytes 8259584 | tf_op jit(solution)/shard_map/reduce_sum | solution.py:32
  390.9 0.0 copy-start.1
  390.9 0.1 copy.52
  391.1 1.1 copy.45
  392.1 4.0 all-to-all-start.2
  396.2 0.0 reduce-scatter.4.cloned.1.call-done
  396.2 1.1 copy.50
  397.3 1.1 copy.46
  398.4 24.2 %all-to-all-done.2 = bf16[8,64,896]{2,1,0:T(8,128)(2,1)S(1)} async-done(((bf16[8,64,896]{2,1,0:T(8,128)(2,1)}), bf16[8,64,896]{2,1,0:T(8,128)(2,1)S(1)}, u32[]{:S(2)}, u32[]{:S(2)}) %all-to-all-start.2) | async-done | bytes 917536 | tf_op jit(solution)/shard_map/all_to_all | solution.py:16
  422.6 0.8 reduce_sum.48
  423.3 0.0 copy-done.1
  (13 shorter events, 0.1 us)
Async XLA Ops:
  7.2 3.2 copy-start
  7.2 133.7 %all-gather.3.cloned.1.call-start = ((), (), s32[]{:S(2)}) async-start(), calls=%async_computation.4 | async-start | bytes 10321920 | tf_op jit(solution)/shard_map/all_gather | solution.py:58
  140.9 7.3 %copy-start.5 = (bf16[32,20,7168]{2,0,1:T(8,128)(2,1)S(1)}, bf16[32,20,7168]{2,0,1:T(8,128)(2,1)}, u32[]{:S(2)}) copy-start(bf16[32,20,7168]{2,0,1:T(8,128)(2,1)} %all-gather.3.cloned.1.call-done) | copy-start | bytes 27525124
  140.9 8.3 %copy-start.6 = (bf16[1,7168,256]{2,1,0:T(8,128)(2,1)S(1)}, bf16[1,7168,256]{2,1,0:T(8,128)(2,1)}, u32[]{:S(2)}) copy-start(bf16[1,7168,256]{2,1,0:T(8,128)(2,1)} %param.11) | copy-start | bytes 11010052
  149.2 2.5 copy-start.2
  170.8 8.1 %copy-start.3 = (bf16[1,1,64,7168]{3,2,1,0:T(8,128)(2,1)S(1)}, bf16[1,1,64,7168]{3,2,1,0:T(8,128)(2,1)}, u32[]{:S(2)}) copy-start(bf16[1,1,64,7168]{3,2,1,0:T(8,128)(2,1)} %param.13) | copy-start | bytes 2752516
  170.8 179.2 %all-to-all-start.1 = ((bf16[32,20,7168]{2,1,0:T(8,128)(2,1)}), bf16[32,20,7168]{2,1,0:T(8,128)(2,1)}, u32[]{:S(2)}, u32[]{:S(2)}) async-start(bf16[32,20,7168]{2,1,0:T(8,128)(2,1)} %copy.43), calls=%async_computation.1 | async-start | bytes 22020096 | tf_op jit(solution)/shard_map/all_to_all | solution.py:76
  178.9 217.3 %reduce-scatter.4.cloned.1.call-start = ((), (), s32[]{:S(2)}) async-start(), calls=%async_computation.5 | async-start | bytes 2064384
  178.9 3.1 copy-start.4
  390.9 32.4 %copy-start.1 = (bf16[64,7168]{1,0:T(8,128)(2,1)S(1)}, bf16[64,7168]{1,0:T(8,128)(2,1)}, u32[]{:S(2)}) copy-start(bf16[64,7168]{1,0:T(8,128)(2,1)} %param.7) | copy-start | bytes 2752516
  392.1 30.4 %all-to-all-start.2 = ((bf16[8,64,896]{2,1,0:T(8,128)(2,1)}), bf16[8,64,896]{2,1,0:T(8,128)(2,1)S(1)}, u32[]{:S(2)}, u32[]{:S(2)}) async-start(bf16[8,64,896]{2,1,0:T(8,128)(2,1)} %copy.45), calls=%async_computation.2 | async-start | bytes 1835008 | tf_op jit(solution)/shard_map/all_to_all | solution.py:16
Sparse Core Ops, SparseCore 0:
  38.2 102.6 all-gather.2
  182.2 35.9 reduce-scatter.3
where the time goes:
time: 431 us; the launch traced here: 430 us
  waiting for transfers between devices  295 us (68%)
  local copies, waits for them, and re-layouts  54.5 us (13%)
  blocking collectives  25.7 us (6%)
  matrix products  17.1 us (4%)
  between operations  14.2 us (3%)
  starting transfers between devices  12.1 us (3%)
  other arithmetic  11.6 us (3%)
    all_to_all x1, waiting for transfers between devices, shards(): lax.all_to_all(partial_out.reshape(experts_all, capacity, width), 'expert...  168 us
    all_gather x1, waiting for transfers between devices, shards(): piece = lax.all_gather(arrived, 'dp', axis=3, tiled=True)  103 us
    all_to_all x1, blocking collectives, shards(): lax.all_to_all(outgoing, 'expert', split_axis=0, concat_axis=0, tiled=True)  25.7 us
    all_to_all x1, waiting for transfers between devices, summed_on_arrival(): lax.all_to_all(blocks, axis, split_axis=0, concat_axis=0, tiled=True)  24.2 us
    gather x1, local copies, waits for them, and re-layouts, combine_rows(): rows = back.reshape(-1, columns)[places]  18.6 us
    reshape x1, local copies, waits for them, and re-layouts, combine_rows(): rows = back.reshape(-1, columns)[places]  13.3 us
    convert_element_type x1, local copies, waits for them, and re-layouts, shards(): partial_out = partial_out.astype(jnp.bfloat16)  13 us
    reduce_sum x1, other arithmetic, combine_rows(): return jnp.sum(weighted.reshape(tok_dev, top, columns), axis=1)  8.91 us
  transfers between devices with their start and end apart: 4, of which 3 were waited for; matrix products, arithmetic and copies ran while one was open for 11% of the time, Pallas kernels for 0%

commit v1 on v0

--- a/solution.py
+++ b/solution.py
@@ -1,9 +1,22 @@
+import functools
 import jax
 import jax.numpy as jnp
 from jax import lax
 from jax.sharding import PartitionSpec as P
 
 HESS_COLS = 128
+
+
+def create_sides(point, bus_axis):
+    return jnp.concatenate(
+        lax.all_to_all(
+            jnp.stack([point] * lax.axis_size(bus_axis)), bus_axis, split_axis=0, concat_axis=0
+        ),
+        axis=3,
+    )
+
+
+shelves_cut = functools.partial(create_sides, bus_axis="dp")
 
 
 def split_up(value, dim, length):
@@ -55,7 +68,7 @@
     outgoing = outgoing.reshape(experts_all, capacity, col_width)
     arrived = lax.all_to_all(outgoing, "expert", split_axis=0, concat_axis=0, tiled=True)
     arrived = arrived.reshape(n_expert, exp_dev, capacity, col_width)
-    piece = lax.all_gather(arrived, "dp", axis=3, tiled=True)
+    piece = shelves_cut(arrived)
     gate_add = jnp.einsum("sjcd,jdf->sjcf", piece, w_gate, preferred_element_type=jnp.float32)
     up_add = jnp.einsum("sjcd,jdf->sjcf", piece, w_up, preferred_element_type=jnp.float32)
     history = prev_inputs.reshape(prev_inputs.shape[1], prev_inputs.shape[2], width)

time: 431 us -> 574 us (1.33); the launches traced: 430 us -> 567 us
  blocking collectives: 25.7 us -> 237 us
  waiting for transfers between devices: 295 us -> 194 us
  local copies, waits for them, and re-layouts: 54.5 us -> 81.2 us
    all_to_all x0 -> x1, blocking collectives: none -> 211 us  [create_sides(): lax.all_to_all(jnp.stack([point] * lax.axis_size(bus_axis)), bus_axis, sp...]
    all_gather x1 -> x0, waiting for transfers between devices: 103 us -> none  [shards(): piece = lax.all_gather(arrived, 'dp', axis=3, tiled=True)]
    another operation x1 -> x3, local copies, waits for them, and re-layouts: 0.01 us -> 15.3 us
    reshape x0 -> x1, local copies, waits for them, and re-layouts: none -> 12.4 us  [create_sides(): jnp.concatenate(lax.all_to_all(jnp.stack([point] * lax.axis_size(bus_axis...]
  transfers between devices with their start and end apart: 4 -> 3, of which waited for: 3 -> 2; matrix products, arithmetic and copies ran while one was open for 11% -> 8% of each run, Pallas kernels for 0% -> 0%
where the time goes in v1:
time: 574 us; the launch traced here: 567 us
  blocking collectives  237 us (41%)
  waiting for transfers between devices  194 us (34%)
  local copies, waits for them, and re-layouts  81.2 us (14%)
  matrix products  17.1 us (3%)
  between operations  14.5 us (3%)
  starting transfers between devices  11.8 us (2%)
  other arithmetic  11.6 us (2%)
    all_to_all x1, blocking collectives, create_sides(): lax.all_to_all(jnp.stack([point] * lax.axis_size(bus_axis)), bus_axis, sp...  211 us
    all_to_all x1, waiting for transfers between devices, shards(): lax.all_to_all(partial_out.reshape(experts_all, capacity, width), 'expert...  169 us
    all_to_all x1, blocking collectives, shards(): lax.all_to_all(outgoing, 'expert', split_axis=0, concat_axis=0, tiled=True)  25.7 us
    all_to_all x1, waiting for transfers between devices, summed_on_arrival(): lax.all_to_all(blocks, axis, split_axis=0, concat_axis=0, tiled=True)  24.1 us
    gather x1, local copies, waits for them, and re-layouts, combine_rows(): rows = back.reshape(-1, columns)[places]  18.8 us
    another operation x2, local copies, waits for them, and re-layouts  14.4 us
    reshape x1, local copies, waits for them, and re-layouts, combine_rows(): rows = back.reshape(-1, columns)[places]  13.3 us
    convert_element_type x1, local copies, waits for them, and re-layouts, shards(): partial_out = partial_out.astype(jnp.bfloat16)  12.8 us
  transfers between devices with their start and end apart: 3, of which 2 were waited for; matrix products, arithmetic and copies ran while one was open for 8% of the time, Pallas kernels for 0%

profile of v1, /device:TPU:13, one launch (start us, length us, event | category | flops | bytes accessed | tf_op | source)
XLA Modules:
  0.0 566.9 jit_solution(2728425536888815909)
XLA Ops:
  7.2 0.0 copy-start
  7.2 0.9 copy.40
  8.0 0.1 eq.44
  8.1 0.1 eq.40
  8.2 1.2 reduce-window.6
  9.4 0.2 slice_reduce_fusion
  9.7 0.1 fusion.28
  9.8 0.1 reduce_sum.44
  9.9 0.5 fusion.8
  10.4 0.0 copy-done
  10.4 0.5 convolution_convert_fusion.1
  10.9 0.3 reshape.132
  11.2 25.7 %all_to_all.20 = bf16[32,20,896]{2,1,0:T(8,128)(2,1)S(1)} all-to-all(bf16[32,20,896]{2,1,0:T(8,128)(2,1)S(1)} %reshape.132), channel_id=1, replica_groups=mesh['dp'=8,'expert'=32] {'expert'}, dimensions={0} | all-to-all | bytes 2293760 | tf_op jit(solution)/shard_map/all_to_all | solution.py:69
  36.9 0.1 copy.44
  37.0 0.9 stack.3
  37.9 211.5 %all_to_all.21 = bf16[8,32,1,20,896]{4,1,3,2,0:T(8,128)(2,1)} all-to-all(bf16[8,32,1,20,896]{4,1,3,2,0:T(8,128)(2,1)S(1)} %stack.3), channel_id=1, replica_groups=mesh['dp'=8,'expert'=32] {'dp'}, dimensions={0} | all-to-all | bytes 18350080 | tf_op jit(solution)/shard_map/all_to_all | solution.py:12
  249.4 12.4 %copy.45 = bf16[32,1,20,8,896]{4,3,0,2,1:T(8,128)(2,1)} copy(bf16[32,1,20,8,896]{4,0,2,1,3:T(8,128)(2,1)} %bitcast.95) | data formatting | bytes 18350080 | tf_op jit(solution)/shard_map/reshape | solution.py:11
  261.8 14.4 %reshape.134 = bf16[32,20,7168]{2,0,1:T(8,128)(2,1)} reshape(bf16[32,1,20,8,896]{4,3,0,2,1:T(8,128)(2,1)} %copy.45) | data formatting | bytes 18350080 | tf_op jit(solution)/shard_map/reshape.5
  276.2 0.0 copy-start.2
  276.2 0.0 copy-start.6
  276.2 7.3 %fusion.9 = f32[32,1,20,256]{3,0,2,1:T(8,128)S(1)} fusion(bf16[32,20,7168]{2,0,1:T(8,128)(2,1)} %reshape.134, bf16[1,7168,256]{2,1,0:T(8,128)(2,1)} %param.10), kind=kOutput, calls=%fused_computation.15 | convolution fusion | flops 2348810240 | bytes 13500416 | tf_op jit(solution)/shard_map/sjcd,jdf->sjcf/dot_general | solution.py:72
  283.5 0.0 copy-done.2
  283.5 0.9 copy-done.6
  284.5 2.5 fusion.21
  287.0 0.0 copy-done.3
  287.0 6.1 %convolution_convert_fusion = bf16[32,20,7168]{2,0,1:T(8,128)(2,1)} fusion(bf16[32,20,256]{2,0,1:T(8,128)(2,1)S(1)} %fusion.21, bf16[1,256,7168]{2,1,0:T(8,128)(2,1)S(1)} %copy-done.3), kind=kOutput, calls=%fused_computation.3 | convolution fusion | flops 2353397760 | bytes 13172736 | tf_op jit(solution)/shard_map/sjcf,jfd->sjcd/dot_general | solution.py:87
  293.1 12.8 %copy.46 = bf16[32,20,7168]{2,1,0:T(8,128)(2,1)} copy(bf16[32,20,7168]{2,0,1:T(8,128)(2,1)} %convolution_convert_fusion) | data formatting | bytes 18350080 | tf_op jit(solution)/shard_map/convert_element_type | solution.py:88
  305.9 8.2 %all-to-all-start.2 = ((bf16[32,20,7168]{2,1,0:T(8,128)(2,1)}), bf16[32,20,7168]{2,1,0:T(8,128)(2,1)}, u32[]{:S(2)}, u32[]{:S(2)}) async-start(bf16[32,20,7168]{2,1,0:T(8,128)(2,1)} %copy.46), calls=%async_computation.2 | async-start | bytes 22020096 | tf_op jit(solution)/shard_map/all_to_all | solution.py:89
  314.1 0.0 reduce-scatter.4.cloned.1.call-start
  314.2 0.0 copy-start.5
  314.2 0.7 fusion.2
  314.9 2.3 copy.52
  317.2 0.0 reduce-scatter.4.cloned.1.call-update
  317.2 0.1 mul.62
  317.3 0.1 copy.47
  317.5 169.5 %all-to-all-done.2 = bf16[32,20,7168]{2,1,0:T(8,128)(2,1)} async-done(((bf16[32,20,7168]{2,1,0:T(8,128)(2,1)}), bf16[32,20,7168]{2,1,0:T(8,128)(2,1)}, u32[]{:S(2)}, u32[]{:S(2)}) %all-to-all-start.2) | async-done | bytes 9175072 | tf_op jit(solution)/shard_map/all_to_all | solution.py:89
  486.9 13.3 %reshape.139 = bf16[640,7168]{1,0:T(8,128)(2,1)} reshape(bf16[32,20,7168]{2,1,0:T(8,128)(2,1)} %all-to-all-done.2) | data formatting | bytes 18350080 | tf_op jit(solution)/shard_map/reshape | solution.py:43
  500.2 18.8 %gather_fusion = bf16[512,7168]{1,0:T(8,128)(2,1)} fusion(bf16[640,7168]{1,0:T(8,128)(2,1)} %reshape.139, s32[1024]{0:T(1024)S(1)} %pad_clamp_fusion), kind=kCustom, calls=%fused_computation | custom fusion | bytes 14682112 | tf_op jit(solution)/shard_map/gather | solution.py:43
  519.0 8.9 %fusion = bf16[64,7168]{1,0:T(8,128)(2,1)S(1)} fusion(bf16[512,7168]{1,0:T(8,128)(2,1)} %gather_fusion, f32[64,8]{1,0:T(8,128)S(1)} %copy.47), kind=kLoop, calls=%fused_computation.2 | loop fusion | flops 10551296 | bytes 8259584 | tf_op jit(solution)/shard_map/reduce_sum | solution.py:45
  527.9 0.0 copy-start.1
  528.0 0.1 copy.55
  528.1 1.1 copy.48
  529.2 3.6 all-to-all-start.3
  532.7 0.0 reduce-scatter.4.cloned.1.call-done
  532.8 1.1 copy.53
  533.9 1.1 copy.49
  535.0 24.1 %all-to-all-done.3 = bf16[8,64,896]{2,1,0:T(8,128)(2,1)S(1)} async-done(((bf16[8,64,896]{2,1,0:T(8,128)(2,1)}), bf16[8,64,896]{2,1,0:T(8,128)(2,1)S(1)}, u32[]{:S(2)}, u32[]{:S(2)}) %all-to-all-start.3) | async-done | bytes 917536 | tf_op jit(solution)/shard_map/all_to_all | solution.py:29
  559.0 0.8 reduce_sum.48
  (14 shorter events, 0.1 us)
Async XLA Ops:
  7.2 3.2 copy-start
  276.2 7.4 %copy-start.2 = (bf16[32,20,7168]{2,0,1:T(8,128)(2,1)S(1)}, bf16[32,20,7168]{2,0,1:T(8,128)(2,1)}, u32[]{:S(2)}) copy-start(bf16[32,20,7168]{2,0,1:T(8,128)(2,1)} %reshape.134) | copy-start | bytes 27525124
  276.2 8.3 %copy-start.6 = (bf16[1,7168,256]{2,1,0:T(8,128)(2,1)S(1)}, bf16[1,7168,256]{2,1,0:T(8,128)(2,1)}, u32[]{:S(2)}) copy-start(bf16[1,7168,256]{2,1,0:T(8,128)(2,1)} %param.11) | copy-start | bytes 11010052
  284.5 2.5 copy-start.3
  305.9 8.2 %copy-start.4 = (bf16[1,1,64,7168]{3,2,1,0:T(8,128)(2,1)S(1)}, bf16[1,1,64,7168]{3,2,1,0:T(8,128)(2,1)}, u32[]{:S(2)}) copy-start(bf16[1,1,64,7168]{3,2,1,0:T(8,128)(2,1)} %param.13) | copy-start | bytes 2752516
  305.9 181.0 %all-to-all-start.2 = ((bf16[32,20,7168]{2,1,0:T(8,128)(2,1)}), bf16[32,20,7168]{2,1,0:T(8,128)(2,1)}, u32[]{:S(2)}, u32[]{:S(2)}) async-start(bf16[32,20,7168]{2,1,0:T(8,128)(2,1)} %copy.46), calls=%async_computation.2 | async-start | bytes 22020096 | tf_op jit(solution)/shard_map/all_to_all | solution.py:89
  314.1 218.6 %reduce-scatter.4.cloned.1.call-start = ((), (), s32[]{:S(2)}) async-start(), calls=%async_computation.5 | async-start | bytes 2064384
  314.2 3.1 copy-start.5
  527.9 31.9 %copy-start.1 = (bf16[64,7168]{1,0:T(8,128)(2,1)S(1)}, bf16[64,7168]{1,0:T(8,128)(2,1)}, u32[]{:S(2)}) copy-start(bf16[64,7168]{1,0:T(8,128)(2,1)} %param.7) | copy-start | bytes 2752516
  529.2 29.9 %all-to-all-start.3 = ((bf16[8,64,896]{2,1,0:T(8,128)(2,1)}), bf16[8,64,896]{2,1,0:T(8,128)(2,1)S(1)}, u32[]{:S(2)}, u32[]{:S(2)}) async-start(bf16[8,64,896]{2,1,0:T(8,128)(2,1)} %copy.48), calls=%async_computation.3 | async-start | bytes 1835008 | tf_op jit(solution)/shard_map/all_to_all | solution.py:29
Sparse Core Ops, SparseCore 0:
  317.5 33.5 reduce-scatter.3
